TPU v7x, 256 devices: a whole 4x4x8 slice. The times are simulated.
256 devices in a mesh: expert: 16 (over x, y), dp: 16 (over z, core).
Axes of the slice: x: 4, y: 4, z: 8, core: 2. Of those that a mesh axis runs over, the one named last changes fastest.
Arguments:
- tokens: bfloat16 [2, 32768, 1280], P(None, ('expert', 'dp')), may hold values from -6 to 6
- modality: int32 [2, 32768], P(None, ('expert', 'dp')), may hold values from 0 to 1, as said below
- routes: int32 [2, 32768, 1], P(None, ('expert', 'dp')), may hold values from 0 to 15; in each aligned block of 128 rows (0 to 127, 128 to 255, ..., all dimensions but the last counted through in order) at most 16 rows name the same one
- router: bfloat16 [1280, 16], replicated, may hold values from -0.15625 to 0.15625
- w_in: bfloat16 [16, 1280, 5120], P('expert', 'dp'), may hold values from -0.15625 to 0.15625
- w_out: bfloat16 [16, 5120, 1280], P('expert', 'dp'), may hold values from -0.078125 to 0.078125
Outputs:
- mixed: bfloat16 [2, 32768, 1280], P(None, ('expert', 'dp'))
- load: float32 [2, 2, 16], replicated
Inputs may be any that keep to these rules, and one draw needn't show every extreme that they name: `routes`: among the 128 tokens of one micro-batch on one device (aligned blocks of 128 rows), at most 16 are routed to any one expert. `modality`: in every aligned block of 128 tokens of a micro-batch, the number of text tokens lies between 32 and 96.
All inputs are finite; a program needn't handle non-finite values.
Results may differ from a plain program's by a relative error of at most 0.0057.
Values may be sent and summed in bfloat16 or wider, within the bound.
No kernel may reach another device: no remote copies, remote signals or barrier semaphores. Data moves between devices by JAX's collectives and lax.ppermute only.
A program may use at most 192 MiB of HBM per device.

v0:
```python
import jax
import jax.numpy as jnp
from jax import lax
from jax.sharding import Mesh
from jax.sharding import PartitionSpec as P

EXPERT = ("expert_0", "expert_1")
DP = ("dp_0", "dp_1")
EXPERT_DP = ("expert_0", "expert_1", "dp_0", "dp_1")


def over_axes(shard, axes):
    for axis in axes:
        shard = lax.psum(shard, axis)
    return shard


def on_device(tokens, modality, routes, router, w_in, w_out):
    micro_count, tok_count, model_width = tokens.shape
    experts = router.shape[1]
    capacity = 2 * tok_count // experts
    logits = jnp.einsum("mtd,de->mte", tokens, router, preferred_element_type=jnp.float32)
    onehot = (routes == jnp.arange(experts, dtype=jnp.int32)[None, None, :]).astype(jnp.float32)
    gating = jax.nn.sigmoid(jnp.sum(logits * onehot, axis=-1))
    running = jnp.cumsum(onehot, axis=1)
    slot_pos = jnp.sum((running - 1.0) * onehot, axis=-1)
    slot_hot = (
        slot_pos[:, :, None] == jnp.arange(capacity, dtype=jnp.float32)[None, None, :]
    ).astype(jnp.float32)
    placer = (onehot[:, :, :, None] * slot_hot[:, :, None, :]).reshape(
        micro_count, tok_count, experts * capacity
    )
    placer = placer.astype(jnp.bfloat16)
    buffer = jnp.einsum("mtk,mtd->mkd", placer, tokens, preferred_element_type=jnp.float32)
    buffer = buffer.astype(jnp.bfloat16).reshape(micro_count, experts, capacity, model_width)
    arrived = lax.all_to_all(buffer, EXPERT, split_axis=1, concat_axis=1, tiled=True)
    token_rows = arrived.reshape(-1, model_width)
    columns = token_rows
    pre_act = jnp.dot(
        columns, lax.all_gather(w_in, DP, axis=1, tiled=True)[0], preferred_element_type=jnp.float32
    )
    hidden = jax.nn.gelu(pre_act, approximate=True).astype(jnp.bfloat16)
    columns = hidden
    served = jnp.dot(
        columns,
        lax.all_gather(w_out, DP, axis=1, tiled=True)[0],
        preferred_element_type=jnp.float32,
    )
    served = served.astype(jnp.bfloat16).reshape(arrived.shape)
    returned = lax.all_to_all(served, EXPERT, split_axis=1, concat_axis=1, tiled=True)
    returned = returned.reshape(micro_count, experts * capacity, model_width)
    combined = jnp.einsum("mtk,mkd->mtd", placer, returned, preferred_element_type=jnp.float32)
    mixed = (combined * gating[:, :, None]).astype(jnp.bfloat16)
    exps = jnp.exp(logits)
    router_probs = exps / jnp.sum(exps, axis=-1, keepdims=True)
    modal_hot = (modality[:, :, None] == jnp.arange(2, dtype=jnp.int32)[None, None, :]).astype(
        jnp.float32
    )
    counts = jnp.einsum("mtk,mte->ke", modal_hot, onehot, precision=lax.Precision.HIGHEST)
    prob_sums = jnp.einsum("mtk,mte->ke", modal_hot, router_probs, precision=lax.Precision.HIGHEST)
    modal_counts = jnp.sum(modal_hot, axis=(0, 1))
    counts, prob_sums, modal_counts = (
        over_axes(counts, EXPERT_DP),
        over_axes(prob_sums, EXPERT_DP),
        over_axes(modal_counts, EXPERT_DP),
    )
    load = jnp.stack(
        [experts * counts / modal_counts[:, None], experts * prob_sums / modal_counts[:, None]]
    )
    return (mixed, load)


def solution(mesh):
    torus = Mesh(mesh.devices.reshape(4, 4, 8, 2), ("expert_0", "expert_1", "dp_0", "dp_1"))
    in_specs = (
        P(None, EXPERT_DP, None),
        P(None, EXPERT_DP),
        P(None, EXPERT_DP, None),
        P(),
        P(EXPERT, DP, None),
        P(EXPERT, DP, None),
    )
    out_specs = (P(None, EXPERT_DP, None), P())
    return jax.shard_map(
        on_device, mesh=torus, in_specs=in_specs, out_specs=out_specs, check_vma=False
    )
```

profile of v0, /device:TPU:1, one launch (start us, length us, event | category | flops | bytes accessed | tf_op | source)
XLA Modules:
  0.0 258.7 jit_solution(4837752513307506845)
XLA Ops:
  7.2 0.0 copy-start
  7.2 0.0 all-gather.5.cloned.1.call-start
  7.2 0.7 all-gather.5.cloned.1.call-update
  7.9 0.0 all-gather.3.cloned.1.call-start
  8.0 0.7 all-gather.3.cloned.1.call-update
  8.7 0.7 fusion.30
  9.3 0.1 copy.21
  9.5 0.2 reduce_window_sum.11
  9.6 0.1 copy.22
  9.7 0.8 fusion.29
  10.5 0.0 copy-done
  10.5 0.5 convolution_convert_fusion
  11.0 0.1 copy.23
  11.1 26.3 %all_to_all.10 = bf16[2,16,16,1280]{3,2,0,1:T(8,128)(2,1)S(1)} all-to-all(bf16[2,16,16,1280]{3,2,0,1:T(8,128)(2,1)S(1)} %copy.23), channel_id=1, replica_groups=mesh['expert_0'=4,'expert_1'=4,'dp_0'=8,'dp_1'=2] {'expert_0','expert_1'}, dimensions={1} | all-to-all | bytes 2621440 | tf_op jit(solution)/shard_map/all_to_all | solution.py:36
  37.5 0.1 copy.24
  37.6 54.6 %all-gather.5.cloned.1.call-done = bf16[1,5120,1280]{2,1,0:T(8,128)(2,1)} async-done(((bf16[1,320,1280]{2,1,0:T(8,128)(2,1)}), bf16[1,5120,1280]{2,1,0:T(8,128)(2,1)}) %all-gather.5.cloned.1.call-update) | async-done | bytes 13107216 | tf_op jit(solution)/shard_map/all_gather | solution.py:46
  92.1 78.5 %all-gather.3.cloned.1.call-done = bf16[1,1280,5120]{2,1,0:T(8,128)(2,1)} async-done(((bf16[1,80,5120]{2,1,0:T(8,128)(2,1)}), bf16[1,1280,5120]{2,1,0:T(8,128)(2,1)}) %all-gather.3.cloned.1.call-update) | async-done | bytes 13107216 | tf_op jit(solution)/shard_map/all_gather | solution.py:40
  170.6 22.4 %fusion.20 = bf16[512,1280]{1,0:T(8,128)(2,1)S(1)} fusion(bf16[1,5120,1280]{2,1,0:T(8,128)(2,1)} %all-gather.5.cloned.1.call-done, bf16[512,1280]{1,0:T(8,128)(2,1)S(1)} %bitcast.41, bf16[1,1280,5120]{2,1,0:T(8,128)(2,1)} %all-gather.3.cloned.1.call-done), kind=kOutput, calls=%fused_computation.17 | convolution fusion | flops 13446021120 | bytes 28835840 | tf_op jit(solution)/shard_map/dot_general | solution.py:44
  193.0 0.0 copy-start.3
  193.0 0.0 copy-start.2
  193.0 0.0 copy-start.1
  193.0 1.2 copy.25
  194.2 6.5 %all-to-all-start.1 = ((bf16[2,16,16,1280]{3,2,0,1:T(8,128)(2,1)}), bf16[2,16,16,1280]{3,2,0,1:T(8,128)(2,1)S(1)}, u32[]{:S(2)}, u32[]{:S(2)}) async-start(bf16[2,16,16,1280]{3,2,0,1:T(8,128)(2,1)} %copy.25), calls=%async_computation.1 | async-start | bytes 2621440 | tf_op jit(solution)/shard_map/all_to_all | solution.py:50
  200.8 0.0 copy-done.3
  200.8 0.1 convert_reduce_fusion
  200.9 0.0 copy-done.2
  200.9 0.1 convolution_bitcast_fusion.1
  201.0 0.0 copy-done.1
  201.0 0.3 exponential_reduce_fusion
  201.4 0.1 convolution_bitcast_fusion
  201.5 18.4 %all-reduce.2 = (f32[2,16]{1,0:T(2,128)S(1)}, f32[2]{0:T(128)S(1)}, f32[2,16]{1,0:T(2,128)S(1)}) all-reduce(f32[2,16]{1,0:T(2,128)S(1)} %convolution_bitcast_fusion, f32[2]{0:T(128)S(1)} %convert_reduce_fusion, f32[2,16]{1,0:T(2,128)S(1)} %convolution_bitcast_fusion.1), channel_id=1, replica_groups=mesh['expert_0'=4,'expert_1'=4,'dp_0'=8,'dp_1'=2] {'expert_0'}, use_global_device_ids=true, to_apply=%region_13.14 | all-reduce | flops 66 | bytes 528 | tf_op jit(solution)/shard_map/psum | solution.py:14
  219.9 8.1 %all-reduce.1 = (f32[2,16]{1,0:T(2,128)S(1)}, f32[2]{0:T(128)S(1)}, f32[2,16]{1,0:T(2,128)S(1)}) all-reduce(f32[2,16]{1,0:T(2,128)S(1)} %get-tuple-element.10, f32[2]{0:T(128)S(1)} %get-tuple-element.11, f32[2,16]{1,0:T(2,128)S(1)} %get-tuple-element.12), channel_id=1, replica_groups=mesh['expert_0'=4,'expert_1'=4,'dp_0'=8,'dp_1'=2] {'expert_1'}, use_global_device_ids=true, to_apply=%region_14.15 | all-reduce | flops 66 | bytes 528 | tf_op jit(solution)/shard_map/psum | solution.py:14
  227.9 11.8 %all-reduce = (f32[2,16]{1,0:T(2,128)S(1)}, f32[2]{0:T(128)S(1)}, f32[2,16]{1,0:T(2,128)S(1)}) all-reduce(f32[2,16]{1,0:T(2,128)S(1)} %get-tuple-element.7, f32[2]{0:T(128)S(1)} %get-tuple-element.8, f32[2,16]{1,0:T(2,128)S(1)} %get-tuple-element.9), channel_id=1, replica_groups=mesh['expert_0'=4,'expert_1'=4,'dp_0'=8,'dp_1'=2] {'dp_0'}, use_global_device_ids=true, to_apply=%region_15.16 | all-reduce | flops 66 | bytes 528 | tf_op jit(solution)/shard_map/psum | solution.py:14
  239.7 10.2 %all-reduce.3 = (f32[2,16]{1,0:T(2,128)S(1)}, f32[2]{0:T(128)S(1)}, f32[2,16]{1,0:T(2,128)S(1)}) all-reduce(f32[2,16]{1,0:T(2,128)S(1)} %get-tuple-element.4, f32[2]{0:T(128)S(1)} %get-tuple-element.5, f32[2,16]{1,0:T(2,128)S(1)} %get-tuple-element.6), channel_id=1, replica_groups=mesh['expert_0'=4,'expert_1'=4,'dp_0'=8,'dp_1'=2] {'dp_1'}, use_global_device_ids=true, to_apply=%region_16.17 | all-reduce | flops 66 | bytes 528 | tf_op jit(solution)/shard_map/psum | solution.py:14
  249.9 0.1 divide_bitcast_fusion.1
  249.9 0.6 pad_maximum_fusion
  250.5 0.0 all-to-all-done.1
  250.5 0.1 copy.26
  250.6 1.2 fusion.25
  (2 shorter events, 0.0 us)
Async XLA Ops:
  7.2 3.3 %copy-start = (bf16[2,128,1280]{2,1,0:T(8,128)(2,1)S(1)}, bf16[2,128,1280]{2,1,0:T(8,128)(2,1)}, u32[]{:S(2)}) copy-start(bf16[2,128,1280]{2,1,0:T(8,128)(2,1)} %param.6) | copy-start | bytes 1966084
  7.2 84.9 %all-gather.5.cloned.1.call-start = ((), (), s32[]{:S(2)}) async-start(), calls=%async_computation.3 | async-start | bytes 13926400 | tf_op jit(solution)/shard_map/all_gather | solution.py:46
  7.9 162.7 %all-gather.3.cloned.1.call-start = ((), (), s32[]{:S(2)}) async-start(), calls=%async_computation.2 | async-start | bytes 13926400 | tf_op jit(solution)/shard_map/all_gather | solution.py:40
  193.0 7.8 %copy-start.3 = (s32[2,128]{1,0:T(2,128)S(1)}, s32[2,128]{1,0:T(2,128)}, u32[]{:S(2)}) copy-start(s32[2,128]{1,0:T(2,128)} %param.7) | copy-start | bytes 3076
  193.0 7.9 %copy-start.2 = (s32[2,128,1]{1,2,0:T(1,128)S(1)}, s32[2,128,1]{1,2,0:T(1,128)}, u32[]{:S(2)}) copy-start(s32[2,128,1]{1,2,0:T(1,128)} %param.8) | copy-start | bytes 3076
  193.0 8.0 %copy-start.1 = (bf16[1280,16]{0,1:T(8,128)(2,1)S(1)}, bf16[1280,16]{0,1:T(8,128)(2,1)}, u32[]{:S(2)}) copy-start(bf16[1280,16]{0,1:T(8,128)(2,1)} %param.9) | copy-start | bytes 122884
  194.2 56.3 %all-to-all-start.1 = ((bf16[2,16,16,1280]{3,2,0,1:T(8,128)(2,1)}), bf16[2,16,16,1280]{3,2,0,1:T(8,128)(2,1)S(1)}, u32[]{:S(2)}, u32[]{:S(2)}) async-start(bf16[2,16,16,1280]{3,2,0,1:T(8,128)(2,1)} %copy.25), calls=%async_computation.1 | async-start | bytes 2621440 | tf_op jit(solution)/shard_map/all_to_all | solution.py:50
Sparse Core Ops, SparseCore 0:
  9.8 82.2 all-gather.4
  93.9 76.5 all-gather.2
where the time goes:
time: 259 us
  waiting for transfers between devices  134 us (52%)
  blocking collectives  74.7 us (29%)
  matrix products  24.7 us (10%)
  between operations  14.2 us (5%)
  starting transfers between devices  6.6 us (3%)
    all_gather x1, waiting for transfers between devices, on_device(): lax.all_gather(w_in, DP, axis=1, tiled=True)[0]  78.5 us
    all_gather x1, waiting for transfers between devices, on_device(): lax.all_gather(w_out, DP, axis=1, tiled=True)[0]  54.6 us
    psum x4, blocking collectives, over_axes(): shard = lax.psum(shard, axis)  48.4 us
    all_to_all x1, blocking collectives, on_device(): lax.all_to_all(buffer, EXPERT, split_axis=1, concat_axis=1, tiled=True)  26.3 us
    dot_general x1, matrix products, on_device(): jnp.dot(columns, lax.all_gather(w_out, DP, axis=1, tiled=True)[0], prefer...  22.4 us
    all_to_all x1, starting transfers between devices, on_device(): lax.all_to_all(served, EXPERT, split_axis=1, concat_axis=1, tiled=True)  6.52 us
  transfers between devices with their start and end apart: 3, of which 2 were waited for; matrix products, arithmetic and copies ran while one was open for 2% of the time, Pallas kernels for 0%

commit v1 on v0

--- a/solution.py
+++ b/solution.py
@@ -1,3 +1,4 @@
+import functools
 import jax
 import jax.numpy as jnp
 from jax import lax
@@ -7,6 +8,15 @@
 EXPERT = ("expert_0", "expert_1")
 DP = ("dp_0", "dp_1")
 EXPERT_DP = ("expert_0", "expert_1", "dp_0", "dp_1")
+
+
+def treat_unit(work_x, dev_axis, dimension_no):
+    odd = jnp.stack(lax.axis_size(dev_axis) * [work_x], 0)
+    current_block = lax.all_to_all(odd, axis_name=dev_axis, split_axis=0, concat_axis=0)
+    return jnp.concatenate(current_block, dimension_no)
+
+
+produce_array = functools.partial(treat_unit, dev_axis=DP, dimension_no=1)
 
 
 def over_axes(shard, axes):
@@ -36,9 +46,7 @@
     arrived = lax.all_to_all(buffer, EXPERT, split_axis=1, concat_axis=1, tiled=True)
     token_rows = arrived.reshape(-1, model_width)
     columns = token_rows
-    pre_act = jnp.dot(
-        columns, lax.all_gather(w_in, DP, axis=1, tiled=True)[0], preferred_element_type=jnp.float32
-    )
+    pre_act = jnp.dot(columns, produce_array(w_in)[0], preferred_element_type=jnp.float32)
     hidden = jax.nn.gelu(pre_act, approximate=True).astype(jnp.bfloat16)
     columns = hidden
     served = jnp.dot(

time: 259 us -> 486 us (1.88)
  waiting for transfers between devices: 134 us -> 346 us
  local copies, waits for them, and re-layouts: 1.69 us -> 9.21 us
  starting transfers between devices: 6.6 us -> 14.1 us
    all_to_all x0 -> x1, waiting for transfers between devices: none -> 345 us  [treat_unit(): lax.all_to_all(odd, axis_name=dev_axis, split_axis=0, concat_axis=0)]
    all_gather x1 -> x0, waiting for transfers between devices: 78.5 us -> none  [on_device(): lax.all_gather(w_in, DP, axis=1, tiled=True)[0]]
    all_gather x1, waiting for transfers between devices: 54.6 us -> 0.01 us  [on_device(): lax.all_gather(w_out, DP, axis=1, tiled=True)[0]]
    all_to_all x0 -> x1, starting transfers between devices: none -> 10.2 us  [treat_unit(): lax.all_to_all(odd, axis_name=dev_axis, split_axis=0, concat_axis=0)]
    another operation x0 -> x1, local copies, waits for them, and re-layouts: none -> 7.51 us  [treat_unit(): odd = jnp.stack(lax.axis_size(dev_axis) * [work_x], 0)]
  transfers between devices with their start and end apart: 3 -> 3, of which waited for: 2 -> 1; matrix products, arithmetic and copies ran while one was open for 2% -> 0% of each run, Pallas kernels for 0% -> 0%
where the time goes in v1:
time: 486 us; the launch traced here: 485 us
  waiting for transfers between devices  346 us (71%)
  blocking collectives  74.9 us (15%)
  matrix products  24.8 us (5%)
  starting transfers between devices  14.1 us (3%)
  between operations  14.1 us (3%)
  local copies, waits for them, and re-layouts  9.21 us (2%)
    all_to_all x1, waiting for transfers between devices, treat_unit(): lax.all_to_all(odd, axis_name=dev_axis, split_axis=0, concat_axis=0)  345 us
    psum x4, blocking collectives, over_axes(): shard = lax.psum(shard, axis)  48.5 us
    all_to_all x1, blocking collectives, on_device(): lax.all_to_all(buffer, EXPERT, split_axis=1, concat_axis=1, tiled=True)  26.3 us
    dot_general x1, matrix products, on_device(): jnp.dot(columns, lax.all_gather(w_out, DP, axis=1, tiled=True)[0], prefer...  22.5 us
    all_to_all x1, starting transfers between devices, treat_unit(): lax.all_to_all(odd, axis_name=dev_axis, split_axis=0, concat_axis=0)  10.2 us
  transfers between devices with their start and end apart: 3, of which 1 were waited for; matrix products, arithmetic and copies ran while one was open for 0% of the time, Pallas kernels for 0%

profile of v1, /device:TPU:1, one launch (start us, length us, event | category | flops | bytes accessed | tf_op | source)
XLA Modules:
  0.0 485.2 jit_solution(8394417171505198803)
XLA Ops:
  7.2 0.0 copy-start
  7.2 0.8 fusion.25
  7.9 0.1 copy.21
  8.0 0.2 reduce_window_sum.11
  8.2 0.1 copy.22
  8.3 0.8 fusion.24
  9.1 0.0 copy-done
  9.1 0.5 convolution_convert_fusion
  9.6 0.1 copy.23
  9.7 26.3 %all_to_all.15 = bf16[2,16,16,1280]{3,2,0,1:T(8,128)(2,1)S(1)} all-to-all(bf16[2,16,16,1280]{3,2,0,1:T(8,128)(2,1)S(1)} %copy.23), channel_id=1, replica_groups=mesh['expert_0'=4,'expert_1'=4,'dp_0'=8,'dp_1'=2] {'expert_0','expert_1'}, dimensions={1} | all-to-all | bytes 2621440 | tf_op jit(solution)/shard_map/all_to_all | solution.py:46
  36.1 7.5 %stack.8 = bf16[16,1,80,5120]{3,2,1,0:T(8,128)(2,1)} broadcast(bf16[80,5120]{1,0:T(8,128)(2,1)} %bitcast.39), dimensions={2,3} | broadcast | bytes 13926400 | tf_op jit(solution)/shard_map/stack | solution.py:14
  43.6 10.2 %all-to-all-start.1 = ((bf16[16,1,80,5120]{3,2,1,0:T(8,128)(2,1)}), bf16[16,1,80,5120]{3,2,1,0:T(8,128)(2,1)}, u32[]{:S(2)}, u32[]{:S(2)}) async-start(bf16[16,1,80,5120]{3,2,1,0:T(8,128)(2,1)} %stack.8), calls=%async_computation.1 | async-start | bytes 26214400 | tf_op jit(solution)/shard_map/all_to_all | solution.py:15
  53.8 0.2 all-gather.2.cloned.1.call-start
  54.0 0.5 all-gather.2.cloned.1.call-update
  54.5 0.1 copy.24
  54.6 345.0 %all-to-all-done.1 = bf16[16,1,80,5120]{3,2,1,0:T(8,128)(2,1)} async-done(((bf16[16,1,80,5120]{3,2,1,0:T(8,128)(2,1)}), bf16[16,1,80,5120]{3,2,1,0:T(8,128)(2,1)}, u32[]{:S(2)}, u32[]{:S(2)}) %all-to-all-start.1) | async-done | bytes 13107232 | tf_op jit(solution)/shard_map/all_to_all | solution.py:15
  399.7 0.0 all-gather.2.cloned.1.call-done
  399.7 0.0 copy-start.3
  399.7 0.0 copy-start.2
  399.7 0.0 copy-start.1
  399.7 22.5 %fusion.15 = bf16[512,1280]{1,0:T(8,128)(2,1)S(1)} fusion(bf16[1,5120,1280]{2,1,0:T(8,128)(2,1)} %all-gather.2.cloned.1.call-done, bf16[512,1280]{1,0:T(8,128)(2,1)S(1)} %bitcast.35, bf16[1280,5120]{1,0:T(8,128)(2,1)} %bitcast.5), kind=kOutput, calls=%fused_computation.15 | convolution fusion | flops 13446021120 | bytes 28835840 | tf_op jit(solution)/shard_map/dot_general | solution.py:52
  422.1 1.2 copy.25
  423.3 3.7 all-to-all-start.2
  427.0 0.0 copy-done.3
  427.1 0.1 convert_reduce_fusion
  427.2 0.0 copy-done.2
  427.2 0.1 convolution_bitcast_fusion.1
  427.3 0.0 copy-done.1
  427.3 0.3 exponential_reduce_fusion
  427.6 0.1 convolution_bitcast_fusion
  427.8 17.7 %all-reduce.2 = (f32[2,16]{1,0:T(2,128)S(1)}, f32[2]{0:T(128)S(1)}, f32[2,16]{1,0:T(2,128)S(1)}) all-reduce(f32[2,16]{1,0:T(2,128)S(1)} %convolution_bitcast_fusion, f32[2]{0:T(128)S(1)} %convert_reduce_fusion, f32[2,16]{1,0:T(2,128)S(1)} %convolution_bitcast_fusion.1), channel_id=1, replica_groups=mesh['expert_0'=4,'expert_1'=4,'dp_0'=8,'dp_1'=2] {'expert_0'}, use_global_device_ids=true, to_apply=%region_13.14 | all-reduce | flops 66 | bytes 528 | tf_op jit(solution)/shard_map/psum | solution.py:24
  445.4 8.6 %all-reduce.1 = (f32[2,16]{1,0:T(2,128)S(1)}, f32[2]{0:T(128)S(1)}, f32[2,16]{1,0:T(2,128)S(1)}) all-reduce(f32[2,16]{1,0:T(2,128)S(1)} %get-tuple-element.10, f32[2]{0:T(128)S(1)} %get-tuple-element.11, f32[2,16]{1,0:T(2,128)S(1)} %get-tuple-element.12), channel_id=1, replica_groups=mesh['expert_0'=4,'expert_1'=4,'dp_0'=8,'dp_1'=2] {'expert_1'}, use_global_device_ids=true, to_apply=%region_14.15 | all-reduce | flops 66 | bytes 528 | tf_op jit(solution)/shard_map/psum | solution.py:24
  454.0 12.3 %all-reduce = (f32[2,16]{1,0:T(2,128)S(1)}, f32[2]{0:T(128)S(1)}, f32[2,16]{1,0:T(2,128)S(1)}) all-reduce(f32[2,16]{1,0:T(2,128)S(1)} %get-tuple-element.7, f32[2]{0:T(128)S(1)} %get-tuple-element.8, f32[2,16]{1,0:T(2,128)S(1)} %get-tuple-element.9), channel_id=1, replica_groups=mesh['expert_0'=4,'expert_1'=4,'dp_0'=8,'dp_1'=2] {'dp_0'}, use_global_device_ids=true, to_apply=%region_15.16 | all-reduce | flops 66 | bytes 528 | tf_op jit(solution)/shard_map/psum | solution.py:24
  466.4 9.9 %all-reduce.3 = (f32[2,16]{1,0:T(2,128)S(1)}, f32[2]{0:T(128)S(1)}, f32[2,16]{1,0:T(2,128)S(1)}) all-reduce(f32[2,16]{1,0:T(2,128)S(1)} %get-tuple-element.4, f32[2]{0:T(128)S(1)} %get-tuple-element.5, f32[2,16]{1,0:T(2,128)S(1)} %get-tuple-element.6), channel_id=1, replica_groups=mesh['expert_0'=4,'expert_1'=4,'dp_0'=8,'dp_1'=2] {'dp_1'}, use_global_device_ids=true, to_apply=%region_16.17 | all-reduce | flops 66 | bytes 528 | tf_op jit(solution)/shard_map/psum | solution.py:24
  476.3 0.1 divide_bitcast_fusion.1
  476.4 0.6 pad_maximum_fusion
  477.0 0.0 all-to-all-done.2
  477.0 0.1 copy.26
  477.1 1.2 fusion.20
  (2 shorter events, 0.0 us)
Async XLA Ops:
  7.2 1.9 copy-start
  43.6 356.1 %all-to-all-start.1 = ((bf16[16,1,80,5120]{3,2,1,0:T(8,128)(2,1)}), bf16[16,1,80,5120]{3,2,1,0:T(8,128)(2,1)}, u32[]{:S(2)}, u32[]{:S(2)}) async-start(bf16[16,1,80,5120]{3,2,1,0:T(8,128)(2,1)} %stack.8), calls=%async_computation.1 | async-start | bytes 26214400 | tf_op jit(solution)/shard_map/all_to_all | solution.py:15
  53.8 345.9 %all-gather.2.cloned.1.call-start = ((), (), s32[]{:S(2)}) async-start(), calls=%async_computation.3 | async-start | bytes 13926400 | tf_op jit(solution)/shard_map/all_gather | solution.py:54
  399.7 27.4 %copy-start.3 = (s32[2,128]{1,0:T(2,128)S(1)}, s32[2,128]{1,0:T(2,128)}, u32[]{:S(2)}) copy-start(s32[2,128]{1,0:T(2,128)} %param.7) | copy-start | bytes 3076
  399.7 27.5 %copy-start.2 = (s32[2,128,1]{1,2,0:T(1,128)S(1)}, s32[2,128,1]{1,2,0:T(1,128)}, u32[]{:S(2)}) copy-start(s32[2,128,1]{1,2,0:T(1,128)} %param.8) | copy-start | bytes 3076
  399.7 27.6 %copy-start.1 = (bf16[1280,16]{0,1:T(8,128)(2,1)S(1)}, bf16[1280,16]{0,1:T(8,128)(2,1)}, u32[]{:S(2)}) copy-start(bf16[1280,16]{0,1:T(8,128)(2,1)} %param.9) | copy-start | bytes 122884
  423.3 53.7 %all-to-all-start.2 = ((bf16[2,16,16,1280]{3,2,0,1:T(8,128)(2,1)}), bf16[2,16,16,1280]{3,2,0,1:T(8,128)(2,1)S(1)}, u32[]{:S(2)}, u32[]{:S(2)}) async-start(bf16[2,16,16,1280]{3,2,0,1:T(8,128)(2,1)} %copy.25), calls=%async_computation.2 | async-start | bytes 2621440 | tf_op jit(solution)/shard_map/all_to_all | solution.py:58
Sparse Core Ops, SparseCore 0:
  56.4 261.9 all-gather.1
